TPU v7x, 32 devices: a whole 2x2x4 slice. The times are simulated.
32 devices in a mesh: rep: 2 (over x), dp: 16 (over y, z, core).
Axes of the slice: x: 2, y: 2, z: 4, core: 2. Of those that a mesh axis runs over, the one named last changes fastest.
Arguments:
- x: bfloat16 [32, 2048, 768], P(('rep', 'dp')), parts along dimension 0
- dy: bfloat16 [32, 2048, 768], P(('rep', 'dp')), parts along dimension 0
- w_gate: bfloat16 [2, 768, 2048], replicated
- w_up: bfloat16 [2, 768, 2048], replicated
- w_down: bfloat16 [2, 2048, 768], replicated
- m_w_gate: float32 [2, 768, 2048], P(None, 'dp')
- m_w_up: float32 [2, 768, 2048], P(None, 'dp')
- m_w_down: float32 [2, 2048, 768], P(None, 'dp')
- v_w_gate: float32 [2, 768, 2048], P(None, 'dp')
- v_w_up: float32 [2, 768, 2048], P(None, 'dp')
- v_w_down: float32 [2, 2048, 768], P(None, 'dp')
Outputs:
- output 1: bfloat16 [4, 768, 2048], P('rep'), parts along dimension 0
- output 2: bfloat16 [4, 768, 2048], P('rep'), parts along dimension 0
- output 3: bfloat16 [4, 2048, 768], P('rep'), parts along dimension 0
- output 4: float32 [4, 768, 2048], P('rep', 'dp'), parts along dimension 0
- output 5: float32 [4, 768, 2048], P('rep', 'dp'), parts along dimension 0
- output 6: float32 [4, 2048, 768], P('rep', 'dp'), parts along dimension 0
- output 7: float32 [4, 768, 2048], P('rep', 'dp'), parts along dimension 0
- output 8: float32 [4, 768, 2048], P('rep', 'dp'), parts along dimension 0
- output 9: float32 [4, 2048, 768], P('rep', 'dp'), parts along dimension 0
There are 2 independent parts. A program takes and returns all parts, laid end to end along the dimension named above; an argument that names none is the same for every part.
All inputs are finite; a program needn't handle non-finite values.
Results may differ from a plain program's by a relative error of at most 0.02.
Values are sent between devices in bfloat16 or wider.
A program may use at most 2 GiB of HBM per device.

v0:
```python
import jax
import jax.numpy as jnp
from jax import lax

NAMES = ("w_gate", "w_up", "w_down")


def matmul(a, w):
    return jnp.dot(a, w, preferred_element_type=jnp.float32).astype(jnp.bfloat16)


def normed(h):
    wide = h.astype(jnp.float32)
    scale = lax.rsqrt(jnp.mean(wide**2, -1, keepdims=True) + 1e-6)
    return (wide * scale).astype(jnp.bfloat16)


def layer(h, w):
    a = normed(h)
    gate = jnp.dot(a, w["w_gate"], preferred_element_type=jnp.float32)
    up = jnp.dot(a, w["w_up"], preferred_element_type=jnp.float32)
    return h + matmul((jax.nn.silu(gate) * up).astype(jnp.bfloat16), w["w_down"])


def adamw(w, m, v, g):
    m = 0.9 * m + 0.1 * g
    v = 0.95 * v + 0.05 * g * g
    step = m * lax.rsqrt(v + 1e-8) + 0.1 * w
    return (w - 0.02 * step).astype(jnp.bfloat16), m, v


def stack(weights, h):
    for number in range(weights["w_gate"].shape[0]):
        h = layer(h, {name: w[number] for name, w in weights.items()})
    return h


def solution(mesh):
    groups = mesh.shape["rep"]

    def step(x, dy, *arrays):
        weights, m, v = (arrays[i : i + 3] for i in (0, 3, 6))
        x, dy = (t.reshape(groups, -1, *t.shape[1:]) for t in (x, dy))

        def of_a_group(x, dy):
            _, back = jax.vjp(lambda w: stack(w, x), dict(zip(NAMES, weights, strict=True)))
            by_weights = back(dy)[0]
            gradients = [by_weights[name].astype(jnp.float32) for name in NAMES]
            new = [adamw(w.astype(jnp.float32), m, v, g) for w, m, v, g in zip(weights, m, v, gradients, strict=True)]
            return tuple(one[which] for which in range(3) for one in new)

        return tuple(t.reshape(-1, *t.shape[2:]) for t in jax.vmap(of_a_group)(x, dy))

    return step
```

profile of v0, /device:TPU:0, one launch (start us, length us, event | category | flops | bytes accessed | tf_op | source)
XLA Modules:
  0.0 1099.4 jit_solution(16150672484023452164)
XLA Ops:
  17.5 11.6 %convolution_convert_fusion.1 = bf16[2048,2048]{1,0:T(8,128)(2,1)} fusion(bf16[1,2048,768]{2,1,0:T(8,128)(2,1)} %param.17, bf16[2,2048,768]{2,1,0:T(8,128)(2,1)} %param.16), kind=kOutput, calls=%fused_computation.208 | convolution fusion | flops 6446645248 | bytes 14680064 | tf_op jit(solution)/vmap(transpose(jvp()))/dot_general | solution.py:9
  29.1 11.8 %fusion.195 = f32[2048,2048]{1,0:T(8,128)} fusion(bf16[2,768,2048]{2,1,0:T(8,128)(2,1)} %param.12, bf16[1,2048,768]{2,1,0:T(8,128)(2,1)S(1)} %copy-done.10, f32[2048]{0:T(1024)S(1)} %add_rsqrt_fusion), kind=kOutput, calls=%fused_computation.238 | convolution fusion | flops 6447169536 | bytes 23076864 | tf_op jit(solution)/vmap(jvp())/dot_general | solution.py:20
  40.9 18.8 %fusion.156 = (bf16[1,1,2048,2048]{3,2,1,0:T(8,128)(2,1)}, f32[2048,2048]{1,0:T(8,128)}) fusion(f32[2048,2048]{1,0:T(8,128)} %fusion.195, bf16[2,768,2048]{2,1,0:T(8,128)(2,1)} %param.15, bf16[1,2048,768]{2,1,0:T(8,128)(2,1)S(1)} %copy-done.10, f32[2048]{0:T(1024)S(1)} %add_rsqrt_fusion), kind=kOutput, calls=%fused_computation.191 | convolution fusion | flops 6472335360 | bytes 48242688 | tf_op jit(solution)/vmap(jvp())/dot_general | solution.py:21
  59.7 12.2 %fusion.166 = (f32[2048]{0:T(1024)S(1)}, bf16[1,1,2048,768]{2,3,1,0:T(8,128)(2,1)S(1)}) fusion(bf16[2,2048,768]{2,1,0:T(8,128)(2,1)} %param.16, bf16[1,1,2048,2048]{3,2,1,0:T(8,128)(2,1)} %get-tuple-element.263, bf16[1,2048,768]{1,2,0:T(8,128)(2,1)} %copy), kind=kOutput, calls=%fused_computation.213 | convolution fusion | flops 6450313216 | bytes 17833984 | tf_op jit(solution)/vmap(jvp())/dot_general | solution.py:9
  74.4 10.0 fusion.184
  84.4 20.9 %fusion.145 = (bf16[1,1,2048,2048]{3,2,1,0:T(8,128)(2,1)}, bf16[1,1,2048,2048]{3,2,1,0:T(8,128)(2,1)}, f32[2048,2048]{1,0:T(8,128)}) fusion(f32[2048,2048]{1,0:T(8,128)S(1)} %fusion.184, bf16[2048,2048]{1,0:T(8,128)(2,1)} %convolution_convert_fusion.1, bf16[2,768,2048]{2,1,0:T(8,128)(2,1)} %param.12, bf16[1,1,2048,768]{2,3,1,0:T(8,128)(2,1)S(1)} %fusion.167), kind=kOutput, calls=%fused_computation.175 | convolution fusion | flops 6505365504 | bytes 65011712 | tf_op jit(solution)/vmap(jvp())/dot_general | solution.py:20
  105.3 11.1 %fusion.155 = bf16[1,1,2048,2048]{3,2,1,0:T(8,128)(2,1)} fusion(f32[2048,2048]{1,0:T(8,128)S(1)} %fusion.184, f32[2048,2048]{1,0:T(8,128)} %get-tuple-element.267), kind=kLoop, calls=%fused_computation.189 | loop fusion | flops 25165824 | bytes 41943040 | tf_op jit(solution)/vmap(jvp())/convert_element_type | solution.py:22
  116.4 12.3 %copy.2 = bf16[1,1,2048,2048]{2,3,1,0:T(8,128)(2,1)} copy(bf16[1,1,2048,2048]{3,2,1,0:T(8,128)(2,1)} %fusion.155) | data formatting | bytes 16777216
  132.0 123.2 %while.16 = (bf16[1,1,2048,2048]{2,3,1,0:T(8,128)(2,1)}, bf16[1,1,2048,768]{3,2,1,0:T(8,128)(2,1)S(1)}, f32[1,128,768]{2,1,0:T(8,128)S(1)}, f32[1,128,768]{2,1,0...) while((bf16[1,1,2048,2048]{2,3,1,0:T(8,128)(2,1)}, ...), condition=%wide.windowed_dot_general_cond_rs.4.clone, body=%wide.windowed_dot_general_body_rs.4.clone.sunk | while | flops 1615396864 | bytes 37225060 | solution.py:9
  255.2 12.8 %copy.4 = bf16[1,1,2048,2048]{2,3,1,0:T(8,128)(2,1)} copy(bf16[1,1,2048,2048]{3,2,1,0:T(8,128)(2,1)} %get-tuple-element.263) | data formatting | bytes 16777216
  268.0 10.2 fusion.172
  278.3 9.6 fusion.168
  293.8 125.2 %while.17 = (bf16[1,1,2048,2048]{2,3,1,0:T(8,128)(2,1)}, bf16[1,1,2048,768]{3,2,1,0:T(8,128)(2,1)}, f32[1,128,768]{2,1,0:T(8,128)S(1)}, f32[1,128,768]{2,1,0:T(8...) while((bf16[1,1,2048,2048]{2,3,1,0:T(8,128)(2,1)}, ...), condition=%wide.windowed_dot_general_cond_rs.5.clone, body=%wide.windowed_dot_general_body_rs.5.clone.sunk | while | flops 1615396864 | bytes 37225060 | solution.py:9
  419.8 121.3 %while.14 = (bf16[1,1,2048,768]{2,3,1,0:T(8,128)(2,1)S(1)}, bf16[1,1,2048,2048]{3,2,1,0:T(8,128)(2,1)}, f32[1,48,2048]{2,1,0:T(8,128)}, f32[1,48,2048]{2,1,0:T(8...) while((bf16[1,1,2048,768]{2,3,1,0:T(8,128)(2,1)S(1)}, ...), condition=%wide.windowed_dot_general_cond_rs.2.clone, body=%wide.windowed_dot_general_body_rs.2.clone.sunk | while | flops 1612775424 | bytes 62390932 | solution.py:21
  472.0 7.0 collective-permute-done.10
  502.6 6.9 collective-permute-done.10
  533.0 7.0 collective-permute-done.10
  545.9 25.1 %convert_multiply_fusion = (bf16[1,1,2048,2048]{3,2,1,0:T(8,128)(2,1)}, bf16[1,1,2048,2048]{3,2,1,0:T(8,128)(2,1)}) fusion(f32[2048,2048]{1,0:T(8,128)} %fusion.195, f32[2048,2048]{1,0:T(8,128)} %get-tuple-element.264, bf16[2,2048,768]{2,1,0:T(8,128)(2,1)} %param.16, bf16[1,1,2048,768]{2,3,1,0:T(8,128)(2,1)} %copy-done.11), kind=kOutput, calls=%fused_computation.170 | convolution fusion | flops 6509559808 | bytes 56623104 | tf_op jit(solution)/vmap(transpose(jvp()))/dot_general | solution.py:9
  571.0 121.1 %while.15 = (bf16[1,1,2048,768]{2,3,1,0:T(8,128)(2,1)}, bf16[1,1,2048,2048]{3,2,1,0:T(8,128)(2,1)}, f32[1,48,2048]{2,1,0:T(8,128)S(1)}, f32[1,48,2048]{2,1,0:T(8...) while((bf16[1,1,2048,768]{2,3,1,0:T(8,128)(2,1)}, ...), condition=%wide.windowed_dot_general_cond_rs.3.clone, body=%wide.windowed_dot_general_body_rs.3.clone.sunk | while | flops 1612775424 | bytes 74973872 | solution.py:21
  592.5 7.4 collective-permute-done.14
  623.0 7.2 collective-permute-done.14
  699.7 150.1 %while.12 = (bf16[1,1,2048,768]{2,3,1,0:T(8,128)(2,1)S(1)}, bf16[1,1,2048,2048]{3,2,1,0:T(8,128)(2,1)}, f32[1,48,2048]{2,1,0:T(8,128)S(1)}, f32[1,48,2048]{2,1,0...) while((bf16[1,1,2048,768]{2,3,1,0:T(8,128)(2,1)S(1)}, ...), condition=%wide.windowed_dot_general_cond_rs.clone, body=%wide.windowed_dot_general_body_rs.clone.sunk | while | flops 1612775424 | bytes 62390932 | solution.py:20
  721.3 9.1 collective-permute-done.2
  760.4 19.9 %collective-permute-start.2 = (f32[1,48,2048]{2,1,0:T(8,128)S(1)}, f32[1,48,2048]{2,1,0:T(8,128)S(1)}, u32[]{:S(2)}, u32[]{:S(2)}) collective-permute-start(f32[1,48,2048]{2,1,0:T(8,128)S(1)} %get-tuple-element.455), channel_id=5, source_target_pairs={{0,1},{1,2},{2,3},{3,4},{4,5},{5,6},{6,7},{7,8},{8,9},{9,10},{10,1... | collective-permute-start | bytes 1179656 | tf_op jit(solution)/vmap(transpose(jvp()))/dot_general | solution.py:20
  811.7 7.9 collective-permute-done.2
  842.0 6.9 collective-permute-done.2
  855.5 145.7 %while.13 = (bf16[1,1,2048,768]{2,3,1,0:T(8,128)(2,1)S(1)}, bf16[1,1,2048,2048]{3,2,1,0:T(8,128)(2,1)}, f32[1,48,2048]{2,1,0:T(8,128)}, f32[1,48,2048]{2,1,0:T(8...) while((bf16[1,1,2048,768]{2,3,1,0:T(8,128)(2,1)S(1)}, ...), condition=%wide.windowed_dot_general_cond_rs.1.clone, body=%wide.windowed_dot_general_body_rs.1.clone.sunk | while | flops 1612775424 | bytes 62390932 | solution.py:20
  876.3 16.3 %collective-permute-done.6 = f32[1,48,2048]{2,1,0:T(8,128)S(1)} collective-permute-done((f32[1,48,2048]{2,1,0:T(8,128)S(1)}, f32[1,48,2048]{2,1,0:T(8,128)S(1)}, u32[]{:S(2)}, u32[]{:S(2)}) %collective-permute-start.6) | collective-permute-done | bytes 393248 | tf_op jit(solution)/vmap(transpose(jvp()))/dot_general | solution.py:20
  916.5 11.9 %collective-permute-start.6 = (f32[1,48,2048]{2,1,0:T(8,128)S(1)}, f32[1,48,2048]{2,1,0:T(8,128)S(1)}, u32[]{:S(2)}, u32[]{:S(2)}) collective-permute-start(f32[1,48,2048]{2,1,0:T(8,128)S(1)} %get-tuple-element.464), channel_id=11, source_target_pairs={{0,1},{1,2},{2,3},{3,4},{4,5},{5,6},{6,7},{7,8},{8,9},{9,10},{10,1... | collective-permute-start | bytes 1179656 | tf_op jit(solution)/vmap(transpose(jvp()))/dot_general | solution.py:20
  1002.2 8.9 collective-permute-done.25
  1015.4 64.0 %all-gather.10.cloned.1.call-done = bf16[1,2,768,2048]{3,2,1,0:T(8,128)(2,1)} async-done(((bf16[1,2,48,2048]{3,2,1,0:T(8,128)(2,1)}), bf16[1,2,768,2048]{3,2,1,0:T(8,128)(2,1)}) %all-gather.10.cloned.1.call-update) | async-done | bytes 6291472 | tf_op jit(solution)/reshape | solution.py:52
  1079.4 7.1 copy.63
  (546 shorter events, 684.0 us)
Async XLA Ops:
  7.2 1008.1 %all-gather.14.cloned.1.call-start = ((), (), s32[]{:S(2)}) async-start(), calls=%async_computation.2 | async-start | bytes 6684672 | tf_op jit(solution)/reshape | solution.py:52
  239.5 13.7 %collective-permute-start.19 = (f32[1,128,768]{2,1,0:T(8,128)S(1)}, f32[1,128,768]{2,1,0:T(8,128)}, u32[]{:S(2)}, u32[]{:S(2)}) collective-permute-start(f32[1,128,768]{2,1,0:T(8,128)S(1)} %get-tuple-element.492), channel_id=30, source_target_pairs={{0,15},{1,0},{2,1},{3,2},{4,3},{5,4},{6,5},{7,6},{8,7},{9,8},{10,9... | collective-permute-start | bytes 1179656 | tf_op jit(solution)/vmap(transpose(jvp()))/dot_general | solution.py:9
  255.2 438.9 %collective-permute-start.28 = (f32[1,128,768]{2,1,0:T(8,128)}, f32[1,128,768]{2,1,0:T(8,128)}, u32[]{:S(2)}, u32[]{:S(2)}) collective-permute-start(f32[1,128,768]{2,1,0:T(8,128)} %get-tuple-element.45), channel_id=32, source_target_pairs={{0,1},{1,2},{2,3},{3,4},{4,5},{5,6},{6,7},{7,8},{8,9},{9,10},{10,1... | collective-permute-start | bytes 1179656 | tf_op jit(solution)/vmap(transpose(jvp()))/dot_general | solution.py:9
  307.8 13.7 %collective-permute-start.22 = (f32[1,128,768]{2,1,0:T(8,128)}, f32[1,128,768]{2,1,0:T(8,128)}, u32[]{:S(2)}, u32[]{:S(2)}) collective-permute-start(f32[1,128,768]{2,1,0:T(8,128)} %get-tuple-element.500), channel_id=37, source_target_pairs={{0,1},{1,2},{2,3},{3,4},{4,5},{5,6},{6,7},{7,8},{8,9},{9,10},{10,1... | collective-permute-start | bytes 1179656 | tf_op jit(solution)/vmap(transpose(jvp()))/dot_general | solution.py:9
  307.8 13.7 %collective-permute-start.23 = (f32[1,128,768]{2,1,0:T(8,128)S(1)}, f32[1,128,768]{2,1,0:T(8,128)}, u32[]{:S(2)}, u32[]{:S(2)}) collective-permute-start(f32[1,128,768]{2,1,0:T(8,128)S(1)} %get-tuple-element.501), channel_id=36, source_target_pairs={{0,15},{1,0},{2,1},{3,2},{4,3},{5,4},{6,5},{7,6},{8,7},{9,8},{10,9... | collective-permute-start | bytes 1179656 | tf_op jit(solution)/vmap(transpose(jvp()))/dot_general | solution.py:9
  371.0 14.0 %collective-permute-start.22 = (f32[1,128,768]{2,1,0:T(8,128)}, f32[1,128,768]{2,1,0:T(8,128)}, u32[]{:S(2)}, u32[]{:S(2)}) collective-permute-start(f32[1,128,768]{2,1,0:T(8,128)} %get-tuple-element.500), channel_id=37, source_target_pairs={{0,1},{1,2},{2,3},{3,4},{4,5},{5,6},{6,7},{7,8},{8,9},{9,10},{10,1... | collective-permute-start | bytes 1179656 | tf_op jit(solution)/vmap(transpose(jvp()))/dot_general | solution.py:9
  371.0 14.0 %collective-permute-start.23 = (f32[1,128,768]{2,1,0:T(8,128)S(1)}, f32[1,128,768]{2,1,0:T(8,128)}, u32[]{:S(2)}, u32[]{:S(2)}) collective-permute-start(f32[1,128,768]{2,1,0:T(8,128)S(1)} %get-tuple-element.501), channel_id=36, source_target_pairs={{0,15},{1,0},{2,1},{3,2},{4,3},{5,4},{6,5},{7,6},{8,7},{9,8},{10,9... | collective-permute-start | bytes 1179656 | tf_op jit(solution)/vmap(transpose(jvp()))/dot_general | solution.py:9
  403.2 13.9 %collective-permute-start.22 = (f32[1,128,768]{2,1,0:T(8,128)}, f32[1,128,768]{2,1,0:T(8,128)}, u32[]{:S(2)}, u32[]{:S(2)}) collective-permute-start(f32[1,128,768]{2,1,0:T(8,128)} %get-tuple-element.500), channel_id=37, source_target_pairs={{0,1},{1,2},{2,3},{3,4},{4,5},{5,6},{6,7},{7,8},{8,9},{9,10},{10,1... | collective-permute-start | bytes 1179656 | tf_op jit(solution)/vmap(transpose(jvp()))/dot_general | solution.py:9
  403.2 13.9 %collective-permute-start.23 = (f32[1,128,768]{2,1,0:T(8,128)S(1)}, f32[1,128,768]{2,1,0:T(8,128)}, u32[]{:S(2)}, u32[]{:S(2)}) collective-permute-start(f32[1,128,768]{2,1,0:T(8,128)S(1)} %get-tuple-element.501), channel_id=36, source_target_pairs={{0,15},{1,0},{2,1},{3,2},{4,3},{5,4},{6,5},{7,6},{8,7},{9,8},{10,9... | collective-permute-start | bytes 1179656 | tf_op jit(solution)/vmap(transpose(jvp()))/dot_general | solution.py:9
  419.0 276.3 %collective-permute-start.29 = (f32[1,128,768]{2,1,0:T(8,128)}, f32[1,128,768]{2,1,0:T(8,128)}, u32[]{:S(2)}, u32[]{:S(2)}) collective-permute-start(f32[1,128,768]{2,1,0:T(8,128)} %get-tuple-element.47), channel_id=38, source_target_pairs={{0,1},{1,2},{2,3},{3,4},{4,5},{5,6},{6,7},{7,8},{8,9},{9,10},{10,1... | collective-permute-start | bytes 1179656 | tf_op jit(solution)/vmap(transpose(jvp()))/dot_general | solution.py:9
  420.7 16.6 %collective-permute-start.8 = (f32[1,48,2048]{2,1,0:T(8,128)}, f32[1,48,2048]{2,1,0:T(8,128)}, u32[]{:S(2)}, u32[]{:S(2)}) collective-permute-start(f32[1,48,2048]{2,1,0:T(8,128)} %broadcast_select_fusion.28), channel_id=16, source_target_pairs={{0,1},{1,2},{2,3},{3,4},{4,5},{5,6},{6,7},{7,8},{8,9},{9,10},{10,1... | collective-permute-start | bytes 1179656 | tf_op jit(solution)/vmap(transpose(jvp()))/dot_general | solution.py:21
  421.5 15.8 %collective-permute-start.9 = (f32[1,48,2048]{2,1,0:T(8,128)}, f32[1,48,2048]{2,1,0:T(8,128)}, u32[]{:S(2)}, u32[]{:S(2)}) collective-permute-start(f32[1,48,2048]{2,1,0:T(8,128)} %broadcast_select_fusion.29), channel_id=15, source_target_pairs={{0,15},{1,0},{2,1},{3,2},{4,3},{5,4},{6,5},{7,6},{8,7},{9,8},{10,9... | collective-permute-start | bytes 1179656 | tf_op jit(solution)/vmap(transpose(jvp()))/dot_general | solution.py:21
  481.8 13.6 %collective-permute-start.8 = (f32[1,48,2048]{2,1,0:T(8,128)}, f32[1,48,2048]{2,1,0:T(8,128)}, u32[]{:S(2)}, u32[]{:S(2)}) collective-permute-start(f32[1,48,2048]{2,1,0:T(8,128)} %broadcast_select_fusion.28), channel_id=16, source_target_pairs={{0,1},{1,2},{2,3},{3,4},{4,5},{5,6},{6,7},{7,8},{8,9},{9,10},{10,1... | collective-permute-start | bytes 1179656 | tf_op jit(solution)/vmap(transpose(jvp()))/dot_general | solution.py:21
  541.0 308.7 %collective-permute-start.26 = (f32[1,48,2048]{2,1,0:T(8,128)}, f32[1,48,2048]{2,1,0:T(8,128)}, u32[]{:S(2)}, u32[]{:S(2)}) collective-permute-start(f32[1,48,2048]{2,1,0:T(8,128)} %get-tuple-element.41), channel_id=19, source_target_pairs={{0,1},{1,2},{2,3},{3,4},{4,5},{5,6},{6,7},{7,8},{8,9},{9,10},{10,1... | collective-permute-start | bytes 1179656 | tf_op jit(solution)/vmap(transpose(jvp()))/dot_general | solution.py:21
  632.8 13.9 %collective-permute-start.12 = (f32[1,48,2048]{2,1,0:T(8,128)}, f32[1,48,2048]{2,1,0:T(8,128)}, u32[]{:S(2)}, u32[]{:S(2)}) collective-permute-start(f32[1,48,2048]{2,1,0:T(8,128)} %broadcast_select_fusion.30), channel_id=22, source_target_pairs={{0,1},{1,2},{2,3},{3,4},{4,5},{5,6},{6,7},{7,8},{8,9},{9,10},{10,1... | collective-permute-start | bytes 1179656 | tf_op jit(solution)/vmap(transpose(jvp()))/dot_general | solution.py:21
  692.1 159.0 %collective-permute-start.27 = (f32[1,48,2048]{2,1,0:T(8,128)}, f32[1,48,2048]{2,1,0:T(8,128)}, u32[]{:S(2)}, u32[]{:S(2)}) collective-permute-start(f32[1,48,2048]{2,1,0:T(8,128)} %get-tuple-element.43), channel_id=25, source_target_pairs={{0,1},{1,2},{2,3},{3,4},{4,5},{5,6},{6,7},{7,8},{8,9},{9,10},{10,1... | collective-permute-start | bytes 1179656 | tf_op jit(solution)/vmap(transpose(jvp()))/dot_general | solution.py:21
  699.6 315.7 %all-gather.12.cloned.1.call-start = ((), (), s32[]{:S(2)}) async-start(), calls=%async_computation.1 | async-start | bytes 6684672 | tf_op jit(solution)/reshape | solution.py:52
  714.8 15.6 %collective-permute-start.2 = (f32[1,48,2048]{2,1,0:T(8,128)S(1)}, f32[1,48,2048]{2,1,0:T(8,128)S(1)}, u32[]{:S(2)}, u32[]{:S(2)}) collective-permute-start(f32[1,48,2048]{2,1,0:T(8,128)S(1)} %get-tuple-element.455), channel_id=5, source_target_pairs={{0,1},{1,2},{2,3},{3,4},{4,5},{5,6},{6,7},{7,8},{8,9},{9,10},{10,1... | collective-permute-start | bytes 1179656 | tf_op jit(solution)/vmap(transpose(jvp()))/dot_general | solution.py:20
  719.8 17.2 %collective-permute-start.3 = (f32[1,48,2048]{2,1,0:T(8,128)S(1)}, f32[1,48,2048]{2,1,0:T(8,128)S(1)}, u32[]{:S(2)}, u32[]{:S(2)}) collective-permute-start(f32[1,48,2048]{2,1,0:T(8,128)S(1)} %get-tuple-element.456), channel_id=4, source_target_pairs={{0,15},{1,0},{2,1},{3,2},{4,3},{5,4},{6,5},{7,6},{8,7},{9,8},{10,9... | collective-permute-start | bytes 1179656 | tf_op jit(solution)/vmap(transpose(jvp()))/dot_general | solution.py:20
  745.6 13.7 %collective-permute-start.1 = (f32[1,48,2048]{2,1,0:T(8,128)}, f32[1,48,2048]{2,1,0:T(8,128)S(1)}, u32[]{:S(2)}, u32[]{:S(2)}) collective-permute-start(f32[1,48,2048]{2,1,0:T(8,128)} %broadcast_select_fusion.25), channel_id=2, source_target_pairs={{0,15},{1,0},{2,1},{3,2},{4,3},{5,4},{6,5},{7,6},{8,7},{9,8},{10,9... | collective-permute-start | bytes 1179656 | tf_op jit(solution)/vmap(transpose(jvp()))/dot_general | solution.py:20
  760.4 22.0 %collective-permute-start.2 = (f32[1,48,2048]{2,1,0:T(8,128)S(1)}, f32[1,48,2048]{2,1,0:T(8,128)S(1)}, u32[]{:S(2)}, u32[]{:S(2)}) collective-permute-start(f32[1,48,2048]{2,1,0:T(8,128)S(1)} %get-tuple-element.455), channel_id=5, source_target_pairs={{0,1},{1,2},{2,3},{3,4},{4,5},{5,6},{6,7},{7,8},{8,9},{9,10},{10,1... | collective-permute-start | bytes 1179656 | tf_op jit(solution)/vmap(transpose(jvp()))/dot_general | solution.py:20
  805.7 13.8 %collective-permute-start.2 = (f32[1,48,2048]{2,1,0:T(8,128)S(1)}, f32[1,48,2048]{2,1,0:T(8,128)S(1)}, u32[]{:S(2)}, u32[]{:S(2)}) collective-permute-start(f32[1,48,2048]{2,1,0:T(8,128)S(1)} %get-tuple-element.455), channel_id=5, source_target_pairs={{0,1},{1,2},{2,3},{3,4},{4,5},{5,6},{6,7},{7,8},{8,9},{9,10},{10,1... | collective-permute-start | bytes 1179656 | tf_op jit(solution)/vmap(transpose(jvp()))/dot_general | solution.py:20
  805.8 13.8 %collective-permute-start.3 = (f32[1,48,2048]{2,1,0:T(8,128)S(1)}, f32[1,48,2048]{2,1,0:T(8,128)S(1)}, u32[]{:S(2)}, u32[]{:S(2)}) collective-permute-start(f32[1,48,2048]{2,1,0:T(8,128)S(1)} %get-tuple-element.456), channel_id=4, source_target_pairs={{0,15},{1,0},{2,1},{3,2},{4,3},{5,4},{6,5},{7,6},{8,7},{9,8},{10,9... | collective-permute-start | bytes 1179656 | tf_op jit(solution)/vmap(transpose(jvp()))/dot_general | solution.py:20
  849.8 151.4 %collective-permute-start.24 = (f32[1,48,2048]{2,1,0:T(8,128)}, f32[1,48,2048]{2,1,0:T(8,128)}, u32[]{:S(2)}, u32[]{:S(2)}) collective-permute-start(f32[1,48,2048]{2,1,0:T(8,128)} %get-tuple-element.37), channel_id=6, source_target_pairs={{0,1},{1,2},{2,3},{3,4},{4,5},{5,6},{6,7},{7,8},{8,9},{9,10},{10,1... | collective-permute-start | bytes 1179656 | tf_op jit(solution)/vmap(transpose(jvp()))/dot_general | solution.py:20
  855.4 224.0 %all-gather.10.cloned.1.call-start = ((), (), s32[]{:S(2)}) async-start(), calls=%async_computation | async-start | bytes 6684672 | tf_op jit(solution)/reshape | solution.py:52
  870.3 22.3 %collective-permute-start.6 = (f32[1,48,2048]{2,1,0:T(8,128)S(1)}, f32[1,48,2048]{2,1,0:T(8,128)S(1)}, u32[]{:S(2)}, u32[]{:S(2)}) collective-permute-start(f32[1,48,2048]{2,1,0:T(8,128)S(1)} %get-tuple-element.464), channel_id=11, source_target_pairs={{0,1},{1,2},{2,3},{3,4},{4,5},{5,6},{6,7},{7,8},{8,9},{9,10},{10,1... | collective-permute-start | bytes 1179656 | tf_op jit(solution)/vmap(transpose(jvp()))/dot_general | solution.py:20
  870.4 22.2 %collective-permute-start.7 = (f32[1,48,2048]{2,1,0:T(8,128)S(1)}, f32[1,48,2048]{2,1,0:T(8,128)S(1)}, u32[]{:S(2)}, u32[]{:S(2)}) collective-permute-start(f32[1,48,2048]{2,1,0:T(8,128)S(1)} %get-tuple-element.465), channel_id=10, source_target_pairs={{0,15},{1,0},{2,1},{3,2},{4,3},{5,4},{6,5},{7,6},{8,7},{9,8},{10,9... | collective-permute-start | bytes 1179656 | tf_op jit(solution)/vmap(transpose(jvp()))/dot_general | solution.py:20
  895.3 13.8 %collective-permute-start.4 = (f32[1,48,2048]{2,1,0:T(8,128)}, f32[1,48,2048]{2,1,0:T(8,128)}, u32[]{:S(2)}, u32[]{:S(2)}) collective-permute-start(f32[1,48,2048]{2,1,0:T(8,128)} %broadcast_select_fusion.26), channel_id=9, source_target_pairs={{0,1},{1,2},{2,3},{3,4},{4,5},{5,6},{6,7},{7,8},{8,9},{9,10},{10,1... | collective-permute-start | bytes 1179656 | tf_op jit(solution)/vmap(transpose(jvp()))/dot_general | solution.py:20
  897.1 18.2 %collective-permute-start.5 = (f32[1,48,2048]{2,1,0:T(8,128)}, f32[1,48,2048]{2,1,0:T(8,128)}, u32[]{:S(2)}, u32[]{:S(2)}) collective-permute-start(f32[1,48,2048]{2,1,0:T(8,128)} %broadcast_select_fusion.27), channel_id=8, source_target_pairs={{0,15},{1,0},{2,1},{3,2},{4,3},{5,4},{6,5},{7,6},{8,7},{9,8},{10,9... | collective-permute-start | bytes 1179656 | tf_op jit(solution)/vmap(transpose(jvp()))/dot_general | solution.py:20
  916.5 18.8 %collective-permute-start.6 = (f32[1,48,2048]{2,1,0:T(8,128)S(1)}, f32[1,48,2048]{2,1,0:T(8,128)S(1)}, u32[]{:S(2)}, u32[]{:S(2)}) collective-permute-start(f32[1,48,2048]{2,1,0:T(8,128)S(1)} %get-tuple-element.464), channel_id=11, source_target_pairs={{0,1},{1,2},{2,3},{3,4},{4,5},{5,6},{6,7},{7,8},{8,9},{9,10},{10,1... | collective-permute-start | bytes 1179656 | tf_op jit(solution)/vmap(transpose(jvp()))/dot_general | solution.py:20
  942.0 13.9 %collective-permute-start.4 = (f32[1,48,2048]{2,1,0:T(8,128)}, f32[1,48,2048]{2,1,0:T(8,128)}, u32[]{:S(2)}, u32[]{:S(2)}) collective-permute-start(f32[1,48,2048]{2,1,0:T(8,128)} %broadcast_select_fusion.26), channel_id=9, source_target_pairs={{0,1},{1,2},{2,3},{3,4},{4,5},{5,6},{6,7},{7,8},{8,9},{9,10},{10,1... | collective-permute-start | bytes 1179656 | tf_op jit(solution)/vmap(transpose(jvp()))/dot_general | solution.py:20
  972.4 13.8 %collective-permute-start.4 = (f32[1,48,2048]{2,1,0:T(8,128)}, f32[1,48,2048]{2,1,0:T(8,128)}, u32[]{:S(2)}, u32[]{:S(2)}) collective-permute-start(f32[1,48,2048]{2,1,0:T(8,128)} %broadcast_select_fusion.26), channel_id=9, source_target_pairs={{0,1},{1,2},{2,3},{3,4},{4,5},{5,6},{6,7},{7,8},{8,9},{9,10},{10,1... | collective-permute-start | bytes 1179656 | tf_op jit(solution)/vmap(transpose(jvp()))/dot_general | solution.py:20
  (135 other events, 1782.3 us)
Sparse Core Ops, SparseCore 0:
  699.8 89.6 all-gather.13
  855.6 84.8 all-gather.11
  1015.4 63.9 all-gather.9
where the time goes:
time: 1110 us; the launch traced here: 1100 us
  waiting for transfers between devices  284 us (26%)
  matrix products  277 us (25%)
  starting transfers between devices  241 us (22%)
  other arithmetic  165 us (15%)
  local copies, waits for them, and re-layouts  69.7 us (6%)
  loops' own time  46.1 us (4%)
  between operations  15.2 us (1%)
    dot_general x34, waiting for transfers between devices, layer(): gate = jnp.dot(a, w['w_gate'], preferred_element_type=jnp.float32)  97.9 us
    dot_general x34, starting transfers between devices, layer(): gate = jnp.dot(a, w['w_gate'], preferred_element_type=jnp.float32)  96.1 us
    dot_general x19, matrix products, layer(): gate = jnp.dot(a, w['w_gate'], preferred_element_type=jnp.float32)  94 us
    dot_general x19, matrix products, matmul(): jnp.dot(a, w, preferred_element_type=jnp.float32).astype(jnp.bfloat16)  91.9 us
    dot_general x19, matrix products, layer(): up = jnp.dot(a, w['w_up'], preferred_element_type=jnp.float32)  91.5 us
    dot_general x34, starting transfers between devices, matmul(): jnp.dot(a, w, preferred_element_type=jnp.float32).astype(jnp.bfloat16)  72.8 us
    dot_general x34, starting transfers between devices, layer(): up = jnp.dot(a, w['w_up'], preferred_element_type=jnp.float32)  72.4 us
    reshape x3, waiting for transfers between devices, step(): t.reshape(-1, *t.shape[2:])  64.1 us
  transfers between devices with their start and end apart: 105, of which 48 were waited for; matrix products, arithmetic and copies ran while one was open for 32% of the time, Pallas kernels for 0%

commit v1 on v0

v1 whole, which is shorter than its diff:
```python
import functools

import jax
import jax.numpy as jnp
from jax import lax
from jax.experimental import pallas as pl
from jax.experimental.pallas import tpu as pltpu
from jax.sharding import PartitionSpec as P

F32, BF16 = jnp.float32, jnp.bfloat16
ANY = pl.BlockSpec(memory_space=pl.ANY)
TOK, D, FF = 2048, 768, 2048
LAYER = (1, 1, 1, 0, 0, 0)
KIND = (0, 1, 2, 0, 1, 2)


def dot(a, b, ca, cb):
    return lax.dot_general(a, b, (((ca,), (cb,)), ((), ())), preferred_element_type=F32)


def loop(lo, hi, f):
    def body(i, carry):
        f(i)
        return carry

    lax.fori_loop(lo, hi, body, 0)


def rows_of(i, size):
    return pl.ds(pl.multiple_of(i * size, size), size)


def norm(h):
    wide = h.astype(F32)
    return (wide * lax.rsqrt(jnp.mean(wide * wide, -1, keepdims=True) + 1e-6)).astype(BF16)


def kernel(
    x_hbm, dy_hbm, wg_hbm, wu_hbm, wd_hbm, mg, mu, md, vg, vu, vd,
    og, ou, od, omg, omu, omd, ovg, ovu, ovd, h1_hbm,
    hid, dgt, dup, abuf, ybuf, bd, bgu, rx1d, rx1gu, rx2d, rx2gu, rx3d, rx3gu, mvd, mvgu, wnd, wngu,
    lsem, hsem, mvsem, mvout, wout, s1, r1, s2, r2, s3, r3, s5, r5, s6, r6, s7, r7, free1, free2,
):
    me = lax.axis_index("dp")
    c = lax.rem(me, 2)
    z = lax.rem(me // 2, 4)
    y = me // 8

    def dev(y, z, c):
        return {"dp": (y * 4 + z) * 2 + c}

    core, across = dev(y, z, 1 - c), dev(1 - y, z, c)
    peers = [lax.rem(z + j, 4) for j in (1, 2, 3)]

    grads = (bd.at[1], bgu.at[0], bgu.at[1], bd.at[0], bgu.at[2], bgu.at[3])
    rx1 = (rx1d, rx1gu.at[0], rx1gu.at[1])
    rx2 = (rx2d, rx2gu.at[0], rx2gu.at[1])
    rx3 = (rx3d, rx3gu.at[0], rx3gu.at[1])
    mv = (mvd, mvgu.at[0], mvgu.at[1])
    wn = (wnd.at[0], wngu.at[0], wngu.at[1], wnd.at[1], wngu.at[2], wngu.at[3])
    out_w, out_m, out_v = (od, og, ou), (omd, omg, omu), (ovd, ovg, ovu)
    in_w, in_m, in_v = (wd_hbm, wg_hbm, wu_hbm), (md, mg, mu), (vd, vg, vu)

    def local(src, dst, sem):
        return pltpu.make_async_copy(src, dst, sem)

    def remote(src, dst, ssem, rsem, to):
        return pltpu.make_async_remote_copy(
            src_ref=src, dst_ref=dst, send_sem=ssem, recv_sem=rsem, device_id=to, device_id_type=pl.DeviceIdType.MESH
        )

    def signal(sem, to):
        pl.semaphore_signal(sem, inc=1, device_id=to, device_id_type=pl.DeviceIdType.MESH)

    def c1(k):
        return remote(grads[k].at[:, :, 1 - c], rx1[k % 3], s1.at[k], r1.at[k], core)

    def c2(k):
        return remote(grads[k].at[1 - y, :, c], rx2[k % 3], s2.at[k], r2.at[k], across)

    def c3(k, j):
        return remote(grads[k].at[y, peers[j], c], rx3[k % 3].at[j], s3.at[k, j], r3.at[k, j], dev(y, peers[j], c))

    def c5(k, j):
        dst = out_w[KIND[k]].at[LAYER[k], y, z, c]
        return remote(wn[k], dst, s5.at[k, j], r5.at[k, j], dev(y, peers[j], c))

    def c6(k):
        part = out_w[KIND[k]].at[LAYER[k], y, :, c]
        return remote(part, part, s6.at[k], r6.at[k], across)

    def c7(k):
        part = out_w[KIND[k]].at[LAYER[k], :, :, c]
        return remote(part, part, s7.at[k], r7.at[k], core)

    def mv_in(k):
        i, layer = k % 3, LAYER[k]
        return [
            local(in_m[i].at[layer], mv[i].at[0], mvsem.at[k, 0]),
            local(in_v[i].at[layer], mv[i].at[1], mvsem.at[k, 1]),
            local(in_w[i].at[layer, y, z, c], wn[k], mvsem.at[k, 2]),
        ]

    def mv_out(k):
        i, layer = k % 3, LAYER[k]
        return [
            local(mv[i].at[0], out_m[i].at[layer], mvout.at[k, 0]),
            local(mv[i].at[1], out_v[i].at[layer], mvout.at[k, 1]),
        ]

    def w_out(k):
        return local(wn[k], out_w[KIND[k]].at[LAYER[k], y, z, c], wout.at[k])

    def t1(k):
        if k >= 3:
            pl.semaphore_wait(free1.at[k % 3], 1)
        c1(k).start()

    def slabs(k):
        return grads[k].shape[-2] // 16

    def t2(k):
        g, a = grads[k], rx1[k % 3]
        c1(k).wait_recv()
        n = slabs(k)

        def add(i):
            zz, r = i // n, rows_of(lax.rem(i, n), 16)
            g[1 - y, zz, c, r, :] = (g[1 - y, zz, c, r, :].astype(F32) + a[1 - y, zz, r, :].astype(F32)).astype(BF16)

        loop(0, 4 * n, add)
        if k >= 3:
            pl.semaphore_wait(free2.at[k % 3], 1)
        c2(k).start()

    def t3(k):
        if k >= 3:
            for copy in mv_out(k - 3):
                copy.wait()
            for copy in mv_in(k):
                copy.start()
        g, a, b = grads[k], rx1[k % 3], rx2[k % 3]
        c2(k).wait_recv()
        n = slabs(k)
        for j in range(3):
            zz = peers[j]

            def add(i):
                r = rows_of(i, 16)
                total = g[y, zz, c, r, :].astype(F32) + a[y, zz, r, :].astype(F32) + b[zz, r, :].astype(F32)
                g[y, zz, c, r, :] = total.astype(BF16)

            loop(0, n, add)
            c3(k, j).start()

    def t4(k):
        g, a, b, d, s, w = grads[k], rx1[k % 3], rx2[k % 3], rx3[k % 3], mv[k % 3], wn[k]
        for copy in mv_in(k):
            copy.wait()
        for j in range(3):
            c3(k, j).wait_recv()

        def step(i):
            r = rows_of(i, 16)
            total = g[y, z, c, r, :].astype(F32) + a[y, z, r, :].astype(F32) + b[z, r, :].astype(F32)
            for j in range(3):
                total += d[j, r, :].astype(F32)
            grad = total.astype(BF16).astype(F32)
            m = 0.9 * s[0, r, :] + 0.1 * grad
            v = 0.95 * s[1, r, :] + 0.05 * grad * grad
            wide = w[r, :].astype(F32)
            s[0, r, :] = m
            s[1, r, :] = v
            w[r, :] = (wide - 0.02 * (m * lax.rsqrt(v + 1e-8) + 0.1 * wide)).astype(BF16)

        loop(0, slabs(k), step)
        for j in range(3):
            c5(k, j).start()
        w_out(k).start()
        for copy in mv_out(k):
            copy.start()
        if k < 3:
            signal(free1.at[k % 3], core)
            signal(free2.at[k % 3], across)

    def t5(k):
        w_out(k).wait()
        for j in range(3):
            c5(k, j).wait_recv()
        c6(k).start()

    def t6(k):
        c6(k).wait_recv()
        c7(k).start()

    def t7(k):
        c7(k).wait_recv()

    def wide_gu(buf, n):
        return buf[:, :, :, :, n].reshape(D, -1)

    def fwd(i):
        m, n = rows_of(i // 8, 1024), rows_of(lax.rem(i, 8), 256)
        am = abuf[m, :]
        gate, up = dot(am, wide_gu(bgu.at[0], n), 1, 0), dot(am, wide_gu(bgu.at[1], n), 1, 0)
        hid[m, n] = (gate * jax.nn.sigmoid(gate) * up).astype(BF16)

    def first(i):
        m = rows_of(i, 512)
        h = ybuf[m, :].astype(F32) + dot(hid[m, :], bd[0].reshape(FF, D), 1, 0).astype(BF16).astype(F32)
        h = h.astype(BF16)
        ybuf[m, :] = h
        abuf[m, :] = norm(h)

    def back(gi, ui, di, tm):
        def unit(i):
            m, n = rows_of(i // 8, tm), rows_of(lax.rem(i, 8), 256)
            b = lax.rem(i, 8)
            am = abuf[m, :]
            gate, up = dot(am, wide_gu(bgu.at[gi], n), 1, 0), dot(am, wide_gu(bgu.at[ui], n), 1, 0)
            wd = bd[di, b // 4, lax.rem(b, 4)].reshape(256, D)
            dh = dot(ybuf[m, :], wd, 1, 1).astype(BF16).astype(F32)
            s = jax.nn.sigmoid(gate)
            act = gate * s
            hid[m, n] = (act * up).astype(BF16)
            dup[m, n] = (dh * act).astype(BF16)
            dgt[m, n] = (dh * up * (s + act * (1.0 - s))).astype(BF16)

        return unit

    def grad_down(k):
        g = grads[k]

        def unit(i):
            n = rows_of(i, 512)
            out = dot(hid[:, n], ybuf[...], 0, 0).astype(BF16)
            g[i // 2, pl.ds(lax.rem(i, 2) * 2, 2)] = out.reshape(2, 2, 128, D)

        return unit

    def grad_gu(k, src):
        g = grads[k]

        def unit(i):
            n = rows_of(i, 512)
            g[:, :, :, :, n] = dot(abuf[...], src[:, n], 0, 0).astype(BF16).reshape(2, 4, 2, 48, 512)

        return unit

    def to_input(i):
        m = rows_of(i, 256)
        from_gate = dot(dgt[m, :], bgu[2].reshape(D, FF), 1, 1).astype(BF16).astype(F32)
        from_up = dot(dup[m, :], bgu[3].reshape(D, FF), 1, 1).astype(BF16).astype(F32)
        da = (from_gate + from_up).astype(BF16).astype(F32)
        h = hid[m, :D].astype(F32)
        scale = lax.rsqrt(jnp.mean(h * h, -1, keepdims=True) + 1e-6)
        dh = da * scale - h * (scale * scale * scale * jnp.mean(da * h, -1, keepdims=True))
        ybuf[m, :] = (ybuf[m, :].astype(F32) + dh.astype(BF16).astype(F32)).astype(BF16)

    def norm_rows(src, dst):
        def unit(i):
            m = rows_of(i, 256)
            dst[m, :] = norm(src[m, :])

        return unit

    load_x = local(x_hbm.at[0], ybuf, lsem.at[0])
    load_w0 = [local(wg_hbm.at[0], bgu.at[0], lsem.at[1]), local(wu_hbm.at[0], bgu.at[1], lsem.at[2]), local(wd_hbm.at[0], bd.at[0], lsem.at[3])]
    load_w1 = [local(wg_hbm.at[1], bgu.at[2], lsem.at[4]), local(wu_hbm.at[1], bgu.at[3], lsem.at[5]), local(wd_hbm.at[1], bd.at[1], lsem.at[6])]
    for copy in [load_x, *load_w0, *load_w1]:
        copy.start()
    barrier = pltpu.get_barrier_semaphore()
    for to in (core, across, *(dev(y, p, c) for p in peers)):
        signal(barrier, to)
    pl.semaphore_wait(barrier, 5)
    for k in range(3):
        for copy in mv_in(k):
            copy.start()

    load_x.wait()
    loop(0, 8, norm_rows(ybuf, abuf))
    load_w0[0].wait()
    load_w0[1].wait()
    loop(0, 16, fwd)
    load_w0[2].wait()
    loop(0, 4, first)
    save_h1 = local(ybuf, h1_hbm, hsem.at[0])
    save_h1.start()
    for copy in load_w1:
        copy.wait()
    save_h1.wait()
    load_dy = local(dy_hbm.at[0], ybuf, hsem.at[1])
    load_dy.start()
    load_dy.wait()
    loop(0, 32, back(2, 3, 1, 512))

    loop(0, 4, grad_down(0))
    t1(0)
    load_h1 = local(h1_hbm, hid.at[:, pl.ds(0, D)], hsem.at[2])
    load_h1.start()
    unit = grad_gu(1, dgt)
    loop(0, 2, unit)
    t2(0)
    loop(2, 4, unit)
    t1(1)
    unit = grad_gu(2, dup)
    loop(0, 2, unit)
    t2(1)
    loop(2, 4, unit)
    t1(2)
    load_x2 = local(x_hbm.at[0], abuf, hsem.at[3])
    load_x2.start()
    load_h1.wait()
    loop(0, 2, to_input)
    t2(2)
    loop(2, 4, to_input)
    t3(0)
    loop(4, 8, to_input)
    reload = [local(wg_hbm.at[0], bgu.at[2], hsem.at[4]), local(wu_hbm.at[0], bgu.at[3], hsem.at[5])]
    for copy in reload:
        copy.start()
    load_x2.wait()
    loop(0, 8, norm_rows(abuf, abuf))
    for copy in reload:
        copy.wait()
    unit = back(2, 3, 0, 512)
    loop(0, 8, unit)
    t3(1)
    loop(8, 16, unit)
    t4(0)
    loop(16, 32, unit)
    t3(2)

    unit = grad_down(3)
    loop(0, 2, unit)
    t4(1)
    loop(2, 4, unit)
    t1(3)
    unit = grad_gu(4, dgt)
    loop(0, 2, unit)
    t2(3)
    loop(2, 4, unit)
    t5(0)
    t1(4)
    unit = grad_gu(5, dup)
    loop(0, 2, unit)
    t2(4)
    loop(2, 4, unit)
    t4(2)
    t1(5)
    t5(1)
    t2(5)
    t6(0)
    t3(3)
    t5(2)
    t6(1)
    t3(4)
    t4(3)
    t6(2)
    t3(5)
    t5(3)
    t4(4)
    t6(3)
    t5(4)
    t4(5)
    t6(4)
    t5(5)
    t6(5)
    for k in range(6):
        t7(k)
        c1(k).wait_send()
        c2(k).wait_send()
        for j in range(3):
            c3(k, j).wait_send()
            c5(k, j).wait_send()
        c6(k).wait_send()
        c7(k).wait_send()
        if k >= 3:
            for copy in mv_out(k):
                copy.wait()


def solution(mesh):
    def step(x, dy, wg, wu, wd, mg, mu, md, vg, vu, vd):
        def split(w):
            return w.reshape(2, 2, 4, 2, -1, w.shape[-1])

        def shape(like, dtype):
            return jax.ShapeDtypeStruct(like.shape, dtype)

        wg6, wu6, wd6 = split(wg), split(wu), split(wd)
        vm = pltpu.VMEM
        dma = pltpu.SemaphoreType.DMA
        outs = pl.pallas_call(
            kernel,
            out_shape=[shape(wg6, BF16), shape(wu6, BF16), shape(wd6, BF16), *(shape(t, F32) for t in (mg, mu, md, vg, vu, vd)),
                       jax.ShapeDtypeStruct((TOK, D), BF16)],
            in_specs=[ANY] * 11,
            out_specs=[ANY] * 10,
            scratch_shapes=[
                vm((TOK, FF), BF16), vm((TOK, FF), BF16), vm((TOK, FF), BF16), vm((TOK, D), BF16), vm((TOK, D), BF16),
                vm((2, 2, 4, 2, 128, D), BF16), vm((4, 2, 4, 2, 48, FF), BF16),
                vm((2, 4, 128, D), BF16), vm((2, 2, 4, 48, FF), BF16),
                vm((4, 128, D), BF16), vm((2, 4, 48, FF), BF16),
                vm((3, 128, D), BF16), vm((2, 3, 48, FF), BF16),
                vm((2, 128, D), F32), vm((2, 2, 48, FF), F32),
                vm((2, 128, D), BF16), vm((4, 48, FF), BF16),
                dma((7,)), dma((6,)), dma((6, 3)), dma((6, 2)), dma((6,)),
                dma((6,)), dma((6,)), dma((6,)), dma((6,)), dma((6, 3)), dma((6, 3)), dma((6, 3)), dma((6, 3)),
                dma((6,)), dma((6,)), dma((6,)), dma((6,)),
                pltpu.SemaphoreType.REGULAR((3,)), pltpu.SemaphoreType.REGULAR((3,)),
            ],
            compiler_params=pltpu.CompilerParams(collective_id=0, has_side_effects=True, vmem_limit_bytes=67043328),
        )(x, dy, wg6, wu6, wd6, mg, mu, md, vg, vu, vd)
        new_w = [o.reshape(w.shape) for o, w in zip(outs[:3], (wg, wu, wd))]
        return (*new_w, *outs[3:9])

    rows = P(None, "dp", None)
    new_rows = P("rep", "dp", None)
    return jax.shard_map(
        step,
        mesh=mesh,
        in_specs=(P(("rep", "dp")), P(("rep", "dp")), P(), P(), P(), *([rows] * 6)),
        out_specs=(P("rep"), P("rep"), P("rep"), *([new_rows] * 6)),
        check_vma=False,
    )
```

time: 1110 us -> 353 us (0.32)
  the two profiles are of different devices: /device:TPU:0 before, /device:TPU:27 now
where the time goes in v1:
time: 353 us
  Pallas kernels  334 us (95%)
  local copies, waits for them, and re-layouts  18.7 us (5%)
    pallas_call x1, Pallas kernels, step(): pl.pallas_call(kernel, out_shape=[shape(wg6, BF16), shape(wu6, BF16), sha...  334 us
    unnamed x27, local copies, waits for them, and re-layouts  18.7 us

profile of v1, /device:TPU:27, one launch (start us, length us, event | category | flops | bytes accessed | tf_op | source)
XLA Modules:
  0.0 353.3 jit_solution(9988854842330159971)
XLA Ops:
  0.6 333.8 %shard_map.178 = (bf16[2,2,4,2,48,2048]{5,4,3,2,1,0:T(8,128)(2,1)}, bf16[2,2,4,2,48,2048]{5,4,3,2,1,0:T(8,128)(2,1)}, bf16[2,2,4,2,128,768]{5,4,3,2,1,0:T(8,128)...) custom-call(bf16[1,2048,768]{2,1,0:T(8,128)(2,1)} %x_hbm.1, ...), custom_call_target="tpu_custom_call" | custom-call | tf_op jit(solution)/shard_map/pallas_call | solution.py:394
  334.5 0.0 copy-start
  334.5 0.0 slice-start
  334.5 7.0 %copy.29 = bf16[2,768,2048]{2,1,0:T(8,128)(2,1)} copy(bf16[2,768,2048]{2,1,0:T(8,128)(2,1)} %bitcast.13) | data formatting | bytes 12582912
  341.6 0.0 copy-done
  341.6 0.0 slice-start.1
  341.6 2.8 copy.30
  344.4 0.0 slice-done
  344.4 0.4 slice-done.1
  344.8 0.0 copy-start.6
  344.8 0.0 copy-start.5
  344.8 0.0 copy-start.4
  344.8 0.0 copy-start.3
  344.8 3.2 copy.31
  348.0 0.0 copy-done.6
  348.0 0.0 copy-start.2
  348.0 0.0 copy-start.1
  348.0 0.9 copy.32
  348.9 0.0 copy-done.5
  348.9 0.9 copy.33
  349.7 0.0 copy-done.4
  349.7 0.9 copy.34
  350.6 0.0 copy-done.3
  350.6 0.9 copy.35
  351.5 0.0 copy-done.2
  351.5 0.9 copy.36
  352.4 0.0 copy-done.1
  352.4 0.9 copy.37
  (1 shorter events, 0.0 us)
Async XLA Ops:
  334.5 7.1 %copy-start = (bf16[2,2,4,2,48,2048]{5,4,3,2,1,0:T(8,128)(2,1)S(1)}, bf16[2,2,4,2,48,2048]{5,4,3,2,1,0:T(8,128)(2,1)}, u32[]{:S(2)}) copy-start(bf16[2,2,4,2,48,2048]{5,4,3,2,1,0:T(8,128)(2,1)} %get-tuple-element.19) | copy-start | bytes 18874372
  334.5 9.9 %slice-start = ((s8[6291456]{0:T(1024)(128)(4,1)}), s8[4194304]{0:T(1024)(128)(4,1)S(1)}, s32[]{:S(2)}) async-start(s8[6291456]{0:T(1024)(128)(4,1)} %bitcast.9), calls=%async_computation | async-start | bytes 8388608
  341.6 3.2 slice-start.1
  344.8 3.2 copy-start.6
  344.8 4.1 %copy-start.5 = (f32[2,48,2048]{2,1,0:T(8,128)S(1)}, f32[2,48,2048]{2,1,0:T(8,128)}, u32[]{:S(2)}) copy-start(f32[2,48,2048]{2,1,0:T(8,128)} %get-tuple-element.40) | copy-start | bytes 2359300
  344.8 5.0 %copy-start.4 = (f32[2,128,768]{2,1,0:T(8,128)S(1)}, f32[2,128,768]{2,1,0:T(8,128)}, u32[]{:S(2)}) copy-start(f32[2,128,768]{2,1,0:T(8,128)} %get-tuple-element.41) | copy-start | bytes 2359300
  344.8 5.9 %copy-start.3 = (f32[2,48,2048]{2,1,0:T(8,128)S(1)}, f32[2,48,2048]{2,1,0:T(8,128)}, u32[]{:S(2)}) copy-start(f32[2,48,2048]{2,1,0:T(8,128)} %get-tuple-element.42) | copy-start | bytes 2359300
  348.0 3.5 %copy-start.2 = (f32[2,48,2048]{2,1,0:T(8,128)S(1)}, f32[2,48,2048]{2,1,0:T(8,128)}, u32[]{:S(2)}) copy-start(f32[2,48,2048]{2,1,0:T(8,128)} %get-tuple-element.43) | copy-start | bytes 2359300
  348.0 4.4 %copy-start.1 = (f32[2,128,768]{2,1,0:T(8,128)S(1)}, f32[2,128,768]{2,1,0:T(8,128)}, u32[]{:S(2)}) copy-start(f32[2,128,768]{2,1,0:T(8,128)} %get-tuple-element.44) | copy-start | bytes 2359300

commit v2 on v1

v2 whole, which is shorter than its diff:
```python
import functools

import jax
import jax.numpy as jnp
from jax import lax
from jax.experimental import pallas as pl
from jax.experimental.pallas import tpu as pltpu
from jax.sharding import PartitionSpec as P

F32, BF16 = jnp.float32, jnp.bfloat16
ANY = pl.BlockSpec(memory_space=pl.ANY)
TOK, D, FF = 2048, 768, 2048
PARTS = (2, 4, 4)
CHUNKS = tuple((layer, kind, part) for layer in (1, 0) for kind in range(3) for part in range(PARTS[kind]))
LAYER, KIND, PART = zip(*CHUNKS)
COUNT = len(CHUNKS)
HALF = COUNT // 2
BY_Y = tuple(way == "y" for way in "yyyyyyyyynyyyyyyynyn")
FROM_Z = tuple(way == "y" for way in "yyynyynyyynynyyynyyy")
BACK = 1024
ORDER = (
    (
        "", "", "", "", "", "c", "gc", "g", "", "", "c", "d", "gdh", "c", "h", "g", "cd", "e", "higec", "di", "g",
        "hc", "e", "f",
    ),
    (
        "ifdgj", "hcej", "if", "d",
    ),
    (
        "ahgb", "ejbiaf", "h", "d", "e", "", "bj", "i",
    ),
    (
        "f", "bad", "eh", "fj", "i", "m", "ambeq", "jfi", "q", "am", "", "nbj", "rfn", "qrma", "b", "j", "q", "omn",
        "osrqa", "s", "", "mnb", "r", "op",
    ),
    (
        "qpmt", "nto", "", "amq",
    ),
)
TAIL = ("lknsroltkpqsnropltsrklopsntklrspotsklpkt", "plktlk",)


def dot(a, b, ca, cb):
    return lax.dot_general(a, b, (((ca,), (cb,)), ((), ())), preferred_element_type=F32)


def loop(lo, hi, f):
    def body(i, carry):
        f(i)
        return carry

    lax.fori_loop(lo, hi, body, 0)


def rows_of(i, size):
    return pl.ds(pl.multiple_of(i * size, size), size)


def norm(h):
    wide = h.astype(F32)
    return (wide * lax.rsqrt(jnp.mean(wide * wide, -1, keepdims=True) + 1e-6)).astype(BF16)


def kernel(
    x_hbm, dy_hbm, wg_hbm, wu_hbm, wd_hbm, mg, mu, md, vg, vu, vd,
    og, ou, od, omg, omu, omd, ovg, ovu, ovd, h1_hbm,
    hid, dgt, dup, abuf, ybuf, bd, bgu, rx1d, rx1gu, rx2d, rx2gu, mvd, mvgu, wnd, wngu,
    lsem, hsem, mvsem, mvout, wout, s1, r1, s2, r2, sa, ra, sb, rb, s5, r5, s6, r6, s7, r7, s8, r8, s9, r9,
    free1, free2, free_a, free_b,
):
    me = lax.axis_index("dp")
    c = lax.rem(me, 2)
    z = lax.rem(me // 2, 4)
    y = me // 8

    def dev(y, z, c):
        return {"dp": (y * 4 + z) * 2 + c}

    core, across = dev(y, z, 1 - c), dev(1 - y, z, c)
    near = z + 1 - 2 * lax.rem(z, 2)
    far = 2 - 2 * (z // 2)
    inner_far = 2 - z // 2
    inner = jnp.logical_or(z == 1, z == 2)
    outer = jnp.logical_or(z == 0, z == 3)

    def cols(k):
        width = (D, FF, FF)[KIND[k]] // PARTS[KIND[k]]
        return pl.ds(PART[k] * width, width)

    def split(refs, dims):
        return tuple(
            ref.at[(*[slice(None)] * dims, cols(k))] for kind, ref in enumerate(refs) for k in range(HALF) if KIND[k] == kind
        )

    whole = (bd.at[1], bgu.at[0], bgu.at[1], bd.at[0], bgu.at[2], bgu.at[3])
    grads = split(whole[:3], 4) + split(whole[3:], 4)
    rx1 = split((rx1d, rx1gu.at[0], rx1gu.at[1]), 3)
    rx2 = split((rx2d, rx2gu.at[0], rx2gu.at[1]), 2)
    mv = split((mvd, mvgu.at[0], mvgu.at[1]), 2)
    wn = split((wnd.at[0], wngu.at[0], wngu.at[1]), 1) + split((wnd.at[1], wngu.at[2], wngu.at[3]), 1)
    out_w, out_m, out_v = (od, og, ou), (omd, omg, omu), (ovd, ovg, ovu)
    in_w, in_m, in_v = (wd_hbm, wg_hbm, wu_hbm), (md, mg, mu), (vd, vg, vu)

    def local(src, dst, sem):
        return pltpu.make_async_copy(src, dst, sem)

    def remote(src, dst, ssem, rsem, to):
        return pltpu.make_async_remote_copy(
            src_ref=src, dst_ref=dst, send_sem=ssem, recv_sem=rsem, device_id=to, device_id_type=pl.DeviceIdType.MESH
        )

    def signal(sem, to):
        pl.semaphore_signal(sem, inc=1, device_id=to, device_id_type=pl.DeviceIdType.MESH)

    def c1(k):
        return remote(grads[k].at[:, :, 1 - c], rx1[k % HALF], s1.at[k], r1.at[k], core)

    def c_y(k):
        if BY_Y[k]:
            return remote(grads[k].at[1 - y, :, c], rx2[k % HALF], s2.at[k], r2.at[k], across)
        return remote(grads[k].at[1 - y, z, c], rx2[k % HALF].at[0], s2.at[k], r2.at[k], across)

    def ys(k):
        return y if BY_Y[k] else slice(None)

    def c_near(k, count):
        which = pl.ds(jnp.where(z == 0, 1, 0), 3) if count == 3 else pl.ds(near, 1)
        g = grads[k]
        return remote(g.at[ys(k), which, c], g.at[ys(k), which, 1 - c], sa.at[k], ra.at[k], dev(y, near, c))

    def c_far(k, i):
        g = grads[k]
        dst = g.at[ys(k), far + 1 - i, 1 - c]
        return remote(g.at[ys(k), far + i, c], dst, sb.at[k, i], rb.at[k], dev(y, far + i, c))

    def place(k):
        return out_w[KIND[k]].at[LAYER[k], :, :, :, :, cols(k)]

    def c_near_w(k, p):
        there = place(k).at[y, z, c] if p == 0 else place(k).at[1 - y, z, c]
        return remote(wn[k] if p == 0 else there, there, s5.at[k, p], r5.at[k, p], dev(y, near, c))

    def c_far_w(k, p, slot=None):
        there = place(k).at[y, z, c] if p == 0 else place(k).at[1 - y, z, c]
        slot = lax.rem(z, 2) if slot is None else slot
        return remote(wn[k] if p == 0 else there, there, s6.at[k, p], r6.at[k, p, slot], dev(y, inner_far, c))

    def c_pass(k):
        part = place(k).at[y if FROM_Z[k] else slice(None), pl.ds(far, 2), c]
        return remote(part, part, s7.at[k], r7.at[k], dev(y, near, c))

    def c_y_w(k):
        if FROM_Z[k]:
            part = place(k).at[y, :, c]
            return remote(part, part, s8.at[k], r8.at[k], across)
        return remote(wn[k], place(k).at[y, z, c], s8.at[k], r8.at[k], across)

    def c_core_w(k):
        part = place(k).at[:, :, c]
        return remote(part, part, s9.at[k], r9.at[k], core)

    def mv_in(k):
        i, layer = KIND[k], LAYER[k]
        return [
            local(in_m[i].at[layer, :, cols(k)], mv[k % HALF].at[0], mvsem.at[k, 0]),
            local(in_v[i].at[layer, :, cols(k)], mv[k % HALF].at[1], mvsem.at[k, 1]),
            local(in_w[i].at[layer, y, z, c, :, cols(k)], wn[k], mvsem.at[k, 2]),
        ]

    def mv_out(k):
        i, layer = KIND[k], LAYER[k]
        return [
            local(mv[k % HALF].at[0], out_m[i].at[layer, :, cols(k)], mvout.at[k, 0]),
            local(mv[k % HALF].at[1], out_v[i].at[layer, :, cols(k)], mvout.at[k, 1]),
        ]

    def w_out(k):
        return local(wn[k], place(k).at[y, z, c], wout.at[k])

    def add_into(k, yy, zz, *more):
        g, a = grads[k], rx1[k % HALF]

        def add(i):
            r = rows_of(i, 16)
            total = g[yy, zz, c, r, :].astype(F32) + a[yy, zz, r, :].astype(F32)
            for ref, at in more:
                total += ref[(*at, r, slice(None))].astype(F32)
            g[yy, zz, c, r, :] = total.astype(BF16)

        loop(0, g.shape[-2] // 16, add)

    def send_core(k):
        if k >= HALF:
            pl.semaphore_wait(free1.at[k % HALF], 1)
        c1(k).start()

    def from_core(k):
        c1(k).wait_recv()
        c1(k).wait_send()
        signal(free_a.at[k], dev(y, near, c))
        signal(free_b.at[k], dev(y, inner_far, c))

    def send_near(k):
        both = (y,) if BY_Y[k] else (0, 1)
        more = [(rx2[k % HALF], None)] if BY_Y[k] else []

        def add(zz):
            for yy in both:
                add_into(k, yy, zz, *((ref, (zz,)) for ref, _ in more))

        pl.semaphore_wait(free_a.at[k], 1)

        @pl.when(outer)
        def _():
            first = jnp.where(z == 0, 1, 0)
            loop(0, 3, lambda i: add(first + i))
            c_near(k, 3).start()

        @pl.when(inner)
        def _():
            add(near)
            c_near(k, 1).start()

    def send_far(k):
        both = (y,) if BY_Y[k] else (0, 1)

        @pl.when(inner)
        def _():
            c_near(k, 3).wait_recv()
            pl.semaphore_wait(free_b.at[k], 2)
            for i in range(2):
                for yy in both:
                    more = [(grads[k], (yy, far + i, 1 - c))]
                    if BY_Y[k]:
                        more.append((rx2[k % HALF], (far + i,)))
                    add_into(k, yy, far + i, *more)
                c_far(k, i).start()

    def from_z(k):
        @pl.when(outer)
        def _():
            c_near(k, 1).wait_recv()

        c_far(k, 0).wait_recv()

    def prefetch(k):
        if k >= HALF:
            for copy in mv_out(k - HALF):
                copy.wait()
            for copy in mv_in(k):
                copy.start()

    def send_y(k):
        if k >= HALF:
            pl.semaphore_wait(free2.at[k % HALF], 1)
        if BY_Y[k]:
            loop(0, 4, lambda zz: add_into(k, 1 - y, zz))
        else:
            add_into(k, 1 - y, z, (grads[k], (1 - y, z, 1 - c)), (grads[k], (1 - y, near, 1 - c)))
        c_y(k).start()

    def update(k):
        g, a, b, s, w = grads[k], rx1[k % HALF], rx2[k % HALF], mv[k % HALF], wn[k]
        for copy in mv_in(k):
            copy.wait()
        kept = z if BY_Y[k] else 0

        def step(i):
            r = rows_of(i, 16)
            total = g[y, z, c, r, :].astype(F32) + a[y, z, r, :].astype(F32) + b[kept, r, :].astype(F32)
            total += g[y, z, 1 - c, r, :].astype(F32) + g[y, near, 1 - c, r, :].astype(F32)
            grad = total.astype(BF16).astype(F32)
            m = 0.9 * s[0, r, :] + 0.1 * grad
            v = 0.95 * s[1, r, :] + 0.05 * grad * grad
            wide = w[r, :].astype(F32)
            s[0, r, :] = m
            s[1, r, :] = v
            w[r, :] = (wide - 0.02 * (m * lax.rsqrt(v + 1e-8) + 0.1 * wide)).astype(BF16)

        loop(0, g.shape[-2] // 16, step)
        if not FROM_Z[k]:
            c_y_w(k).start()
        c_near_w(k, 0).start()
        c_far_w(k, 0).start()
        w_out(k).start()
        for copy in mv_out(k):
            copy.start()
        if k < HALF:
            signal(free1.at[k % HALF], core)
            signal(free2.at[k % HALF], across)

    def pass_on(k, parts):
        @pl.when(inner)
        def _():
            for p in range(parts):
                c_near_w(k, p).wait_recv()
                for slot in range(2):
                    c_far_w(k, p, slot).wait_recv()
            c_pass(k).start()

    def gathered_z(k, parts):
        @pl.when(outer)
        def _():
            for p in range(parts):
                c_near_w(k, p).wait_recv()
            c_pass(k).wait_recv()

    def steps(k):
        def second():
            from_core(k)
            send_y(k) if BY_Y[k] else send_near(k)

        def third():
            prefetch(k)
            if BY_Y[k]:
                c_y(k).wait_recv()
                send_near(k)
            else:
                send_far(k)

        def fourth():
            if BY_Y[k]:
                send_far(k)
            else:
                from_z(k)
                send_y(k)

        def fifth():
            if BY_Y[k]:
                from_z(k)
            else:
                c_y(k).wait_recv()
            update(k)

        def sixth():
            if FROM_Z[k]:
                pass_on(k, 1)
            else:
                c_y_w(k).wait_recv()
                c_near_w(k, 1).start()
                c_far_w(k, 1).start()

        def seventh():
            if FROM_Z[k]:
                w_out(k).wait()
                gathered_z(k, 1)
                c_y_w(k).start()
            else:
                pass_on(k, 2)

        def eighth():
            if FROM_Z[k]:
                c_y_w(k).wait_recv()
            else:
                w_out(k).wait()
                gathered_z(k, 2)
            c_core_w(k).start()

        return lambda: send_core(k), second, third, fourth, fifth, sixth, seventh, eighth

    def wide_gu(buf, n):
        return buf[:, :, :, :, n].reshape(D, -1)

    def fwd(i):
        m, n = rows_of(i // 8, 1024), rows_of(lax.rem(i, 8), 256)
        am = abuf[m, :]
        gate, up = dot(am, wide_gu(bgu.at[0], n), 1, 0), dot(am, wide_gu(bgu.at[1], n), 1, 0)
        hid[m, n] = (gate * jax.nn.sigmoid(gate) * up).astype(BF16)

    def first(i):
        m = rows_of(i, 512)
        h = ybuf[m, :].astype(F32) + dot(hid[m, :], bd[0].reshape(FF, D), 1, 0).astype(BF16).astype(F32)
        h = h.astype(BF16)
        ybuf[m, :] = h
        abuf[m, :] = norm(h)

    def back(gi, ui, di, tm):
        def unit(i):
            b = i // (TOK // tm)
            m, n = rows_of(lax.rem(i, TOK // tm), tm), rows_of(b, 256)
            am = abuf[m, :]
            gate, up = dot(am, wide_gu(bgu.at[gi], n), 1, 0), dot(am, wide_gu(bgu.at[ui], n), 1, 0)
            wd = bd[di, b // 4, lax.rem(b, 4)].reshape(256, D)
            dh = dot(ybuf[m, :], wd, 1, 1).astype(BF16).astype(F32)
            s = jax.nn.sigmoid(gate)
            act = gate * s
            hid[m, n] = (act * up).astype(BF16)
            dup[m, n] = (dh * act).astype(BF16)
            dgt[m, n] = (dh * up * (s + act * (1.0 - s))).astype(BF16)

        return unit

    def grad_down(k):
        g = whole[k]

        def unit(i):
            n = rows_of(i, 512)
            out = dot(hid[:, n], ybuf[...], 0, 0).astype(BF16)
            g[i // 2, pl.ds(lax.rem(i, 2) * 2, 2)] = out.reshape(2, 2, 128, D)

        return unit

    def grad_gu(k, src):
        g = whole[k]

        def unit(i):
            n = rows_of(i, 512)
            g[:, :, :, :, n] = dot(abuf[...], src[:, n], 0, 0).astype(BF16).reshape(2, 4, 2, 48, 512)

        return unit

    def to_input(i):
        m = rows_of(i, 256)
        from_gate = dot(dgt[m, :], bgu[2].reshape(D, FF), 1, 1).astype(BF16).astype(F32)
        from_up = dot(dup[m, :], bgu[3].reshape(D, FF), 1, 1).astype(BF16).astype(F32)
        da = (from_gate + from_up).astype(BF16).astype(F32)
        h = hid[m, :D].astype(F32)
        scale = lax.rsqrt(jnp.mean(h * h, -1, keepdims=True) + 1e-6)
        dh = da * scale - h * (scale * scale * scale * jnp.mean(da * h, -1, keepdims=True))
        ybuf[m, :] = (ybuf[m, :].astype(F32) + dh.astype(BF16).astype(F32)).astype(BF16)

    def norm_rows(src, dst):
        def unit(i):
            m = rows_of(i, 256)
            dst[m, :] = norm(src[m, :])

        return unit

    load_x = local(x_hbm.at[0], ybuf, lsem.at[0])
    load_w0 = [local(wg_hbm.at[0], bgu.at[0], lsem.at[1]), local(wu_hbm.at[0], bgu.at[1], lsem.at[2]), local(wd_hbm.at[0], bd.at[0], lsem.at[3])]
    load_w1 = [local(wg_hbm.at[1], bgu.at[2], lsem.at[4]), local(wu_hbm.at[1], bgu.at[3], lsem.at[5]), local(wd_hbm.at[1], bd.at[1], lsem.at[6])]
    for copy in [load_x, *load_w0, *load_w1]:
        copy.start()
    barrier = pltpu.get_barrier_semaphore()
    for to in (core, across, *(dev(y, lax.rem(z + j, 4), c) for j in (1, 2, 3))):
        signal(barrier, to)
    pl.semaphore_wait(barrier, 5)
    for k in range(HALF):
        for copy in mv_in(k):
            copy.start()

    load_x.wait()
    loop(0, 8, norm_rows(ybuf, abuf))
    load_w0[0].wait()
    load_w0[1].wait()
    loop(0, 16, fwd)
    load_w0[2].wait()
    loop(0, 4, first)
    save_h1 = local(ybuf, h1_hbm, hsem.at[0])
    save_h1.start()
    for copy in load_w1:
        copy.wait()
    save_h1.wait()
    load_dy = local(dy_hbm.at[0], ybuf, hsem.at[1])
    load_dy.start()
    load_dy.wait()

    load_h1 = local(h1_hbm, hid.at[:, pl.ds(0, D)], hsem.at[2])
    load_x2 = local(x_hbm.at[0], abuf, hsem.at[3])
    reload = [local(wg_hbm.at[0], bgu.at[2], hsem.at[4]), local(wu_hbm.at[0], bgu.at[3], hsem.at[5])]

    def before_input():
        load_x2.start()
        load_h1.start()
        load_h1.wait()

    def before_back():
        for copy in reload:
            copy.start()
        load_x2.wait()
        loop(0, 8, norm_rows(abuf, abuf))
        for copy in reload:
            copy.wait()

    left = [list(steps(k)) for k in range(COUNT)]

    def listed(letters):
        return [left[ord(letter) - ord("a")].pop(0) for letter in letters]

    plan = [[listed(letters) for letters in product] for product in ORDER]
    rest = listed("".join(TAIL))
    assert not any(left)

    def run(todo):
        for step in todo:
            step()

    def between(product, i, which):
        for at in which:
            if at and plan[product][at]:
                pl.when(i == at)(functools.partial(run, plan[product][at]))

    def plain(product, unit):
        def piece(i):
            between(product, i, range(len(ORDER[product])))
            unit(i)

        loop(0, len(ORDER[product]), piece)

    def by_quarters(product, unit, gate, up):
        each = len(ORDER[product]) // 4

        def quarter(q):
            def piece(j):
                between(product, q * each + j, [at for at in range(4 * each) if at % each < each - 2])
                unit(q * (each - 2) + j)

            loop(0, each - 2, piece)
            for last, grad in ((2, gate), (1, up)):
                for at in range(each - last, 4 * each, each):
                    if plan[product][at]:
                        pl.when(q == at // each)(functools.partial(run, plan[product][at]))
                grad(q)

        loop(0, 4, quarter)

    run(plan[0][0])
    by_quarters(0, back(2, 3, 1, BACK), grad_gu(1, dgt), grad_gu(2, dup))
    run(plan[1][0])
    plain(1, grad_down(0))
    run(plan[2][0])
    before_input()
    plain(2, to_input)
    run(plan[3][0])
    before_back()
    by_quarters(3, back(2, 3, 0, BACK), grad_gu(4, dgt), grad_gu(5, dup))
    run(plan[4][0])
    plain(4, grad_down(3))
    run(rest)

    for k in range(COUNT):
        c_core_w(k).wait_recv()
        c_y(k).wait_send()
        c_near_w(k, 0).wait_send()
        c_far_w(k, 0).wait_send()
        if not FROM_Z[k]:
            c_near_w(k, 1).wait_send()
            c_far_w(k, 1).wait_send()
        c_y_w(k).wait_send()
        c_core_w(k).wait_send()
        if k >= HALF:
            for copy in mv_out(k):
                copy.wait()

    @pl.when(outer)
    def _():
        for k in range(COUNT):
            c_near(k, 3).wait_send()

    @pl.when(inner)
    def _():
        for k in range(COUNT):
            c_near(k, 1).wait_send()
            c_pass(k).wait_send()
            for i in range(2):
                c_far(k, i).wait_send()


def solution(mesh):
    def step(x, dy, wg, wu, wd, mg, mu, md, vg, vu, vd):
        def split(w):
            return w.reshape(2, 2, 4, 2, -1, w.shape[-1])

        def shape(like, dtype):
            return jax.ShapeDtypeStruct(like.shape, dtype)

        wg6, wu6, wd6 = split(wg), split(wu), split(wd)
        vm = pltpu.VMEM
        dma = pltpu.SemaphoreType.DMA
        outs = pl.pallas_call(
            kernel,
            out_shape=[shape(wg6, BF16), shape(wu6, BF16), shape(wd6, BF16), *(shape(t, F32) for t in (mg, mu, md, vg, vu, vd)),
                       jax.ShapeDtypeStruct((TOK, D), BF16)],
            in_specs=[ANY] * 11,
            out_specs=[ANY] * 10,
            scratch_shapes=[
                vm((TOK, FF), BF16), vm((TOK, FF), BF16), vm((TOK, FF), BF16), vm((TOK, D), BF16), vm((TOK, D), BF16),
                vm((2, 2, 4, 2, 128, D), BF16), vm((4, 2, 4, 2, 48, FF), BF16),
                vm((2, 4, 128, D), BF16), vm((2, 2, 4, 48, FF), BF16),
                vm((4, 128, D), BF16), vm((2, 4, 48, FF), BF16),
                vm((2, 128, D), F32), vm((2, 2, 48, FF), F32),
                vm((2, 128, D), BF16), vm((4, 48, FF), BF16),
                dma((7,)), dma((6,)), dma((COUNT, 3)), dma((COUNT, 2)), dma((COUNT,)),
                *([dma((COUNT,))] * 6), dma((COUNT, 2)), dma((COUNT,)),
                dma((COUNT, 2)), dma((COUNT, 2)), dma((COUNT, 2)), dma((COUNT, 2, 2)), *([dma((COUNT,))] * 6),
                *(pltpu.SemaphoreType.REGULAR((n,)) for n in (HALF, HALF, COUNT, COUNT)),
            ],
            compiler_params=pltpu.CompilerParams(collective_id=0, has_side_effects=True, vmem_limit_bytes=67043328),
        )(x, dy, wg6, wu6, wd6, mg, mu, md, vg, vu, vd)
        new_w = [o.reshape(w.shape) for o, w in zip(outs[:3], (wg, wu, wd))]
        return (*new_w, *outs[3:9])

    rows = P(None, "dp", None)
    new_rows = P("rep", "dp", None)
    return jax.shard_map(
        step,
        mesh=mesh,
        in_specs=(P(("rep", "dp")), P(("rep", "dp")), P(), P(), P(), *([rows] * 6)),
        out_specs=(P("rep"), P("rep"), P("rep"), *([new_rows] * 6)),
        check_vma=False,
    )
```

time: 353 us -> 267 us (0.76)
  the two profiles are of different devices: /device:TPU:27 before, /device:TPU:0 now
where the time goes in v2:
time: 267 us
  Pallas kernels  247 us (93%)
  local copies, waits for them, and re-layouts  18.7 us (7%)
    pallas_call x1, Pallas kernels, step(): pl.pallas_call(kernel, out_shape=[shape(wg6, BF16), shape(wu6, BF16), sha...  247 us
    unnamed x27, local copies, waits for them, and re-layouts  18.7 us

profile of v2, /device:TPU:0, one launch (start us, length us, event | category | flops | bytes accessed | tf_op | source)
XLA Modules:
  0.0 266.8 jit_solution(8630400860572736539)
XLA Ops:
  0.6 247.4 %shard_map.178 = (bf16[2,2,4,2,48,2048]{5,4,3,2,1,0:T(8,128)(2,1)}, bf16[2,2,4,2,48,2048]{5,4,3,2,1,0:T(8,128)(2,1)}, bf16[2,2,4,2,128,768]{5,4,3,2,1,0:T(8,128)...) custom-call(bf16[1,2048,768]{2,1,0:T(8,128)(2,1)} %x_hbm.1, ...), custom_call_target="tpu_custom_call" | custom-call | tf_op jit(solution)/shard_map/pallas_call | solution.py:570
  248.1 0.0 copy-start
  248.1 0.0 slice-start
  248.1 7.0 %copy.29 = bf16[2,768,2048]{2,1,0:T(8,128)(2,1)} copy(bf16[2,768,2048]{2,1,0:T(8,128)(2,1)} %bitcast.13) | data formatting | bytes 12582912
  255.1 0.0 copy-done
  255.1 0.0 slice-start.1
  255.1 2.8 %copy.30 = bf16[2,768,2048]{2,1,0:T(8,128)(2,1)} copy(bf16[2,768,2048]{2,1,0:T(8,128)(2,1)S(1)} %bitcast.12) | data formatting | bytes 12582912
  257.9 0.0 slice-done
  257.9 0.4 slice-done.1
  258.3 0.0 copy-start.6
  258.3 0.0 copy-start.5
  258.3 0.0 copy-start.4
  258.3 0.0 copy-start.3
  258.3 3.2 %copy.31 = bf16[2,2048,768]{2,1,0:T(8,128)(2,1)} copy(bf16[2,2048,768]{2,1,0:T(8,128)(2,1)S(1)} %bitcast.11) | data formatting | bytes 12582912
  261.5 0.0 copy-done.6
  261.5 0.0 copy-start.2
  261.5 0.0 copy-start.1
  261.5 0.9 copy.32
  262.4 0.0 copy-done.5
  262.4 0.9 copy.33
  263.3 0.0 copy-done.4
  263.3 0.9 copy.34
  264.2 0.0 copy-done.3
  264.2 0.9 copy.35
  265.1 0.0 copy-done.2
  265.1 0.9 copy.36
  265.9 0.0 copy-done.1
  265.9 0.9 copy.37
  (1 shorter events, 0.0 us)
Async XLA Ops:
  248.1 7.1 %copy-start = (bf16[2,2,4,2,48,2048]{5,4,3,2,1,0:T(8,128)(2,1)S(1)}, bf16[2,2,4,2,48,2048]{5,4,3,2,1,0:T(8,128)(2,1)}, u32[]{:S(2)}) copy-start(bf16[2,2,4,2,48,2048]{5,4,3,2,1,0:T(8,128)(2,1)} %get-tuple-element.19) | copy-start | bytes 18874372
  248.1 9.9 %slice-start = ((s8[6291456]{0:T(1024)(128)(4,1)}), s8[4194304]{0:T(1024)(128)(4,1)S(1)}, s32[]{:S(2)}) async-start(s8[6291456]{0:T(1024)(128)(4,1)} %bitcast.9), calls=%async_computation | async-start | bytes 8388608
  255.1 3.2 %slice-start.1 = ((s8[6291456]{0:T(1024)(128)(4,1)}), s8[2097152]{0:T(1024)(128)(4,1)S(1)}, s32[]{:S(2)}) async-start(s8[6291456]{0:T(1024)(128)(4,1)} %bitcast.9), calls=%async_computation.1 | async-start | bytes 4194304
  258.3 3.2 %copy-start.6 = (f32[2,48,2048]{2,1,0:T(8,128)S(1)}, f32[2,48,2048]{2,1,0:T(8,128)}, u32[]{:S(2)}) copy-start(f32[2,48,2048]{2,1,0:T(8,128)} %get-tuple-element.39) | copy-start | bytes 2359300
  258.3 4.1 %copy-start.5 = (f32[2,48,2048]{2,1,0:T(8,128)S(1)}, f32[2,48,2048]{2,1,0:T(8,128)}, u32[]{:S(2)}) copy-start(f32[2,48,2048]{2,1,0:T(8,128)} %get-tuple-element.40) | copy-start | bytes 2359300
  258.3 5.0 %copy-start.4 = (f32[2,128,768]{2,1,0:T(8,128)S(1)}, f32[2,128,768]{2,1,0:T(8,128)}, u32[]{:S(2)}) copy-start(f32[2,128,768]{2,1,0:T(8,128)} %get-tuple-element.41) | copy-start | bytes 2359300
  258.3 5.9 %copy-start.3 = (f32[2,48,2048]{2,1,0:T(8,128)S(1)}, f32[2,48,2048]{2,1,0:T(8,128)}, u32[]{:S(2)}) copy-start(f32[2,48,2048]{2,1,0:T(8,128)} %get-tuple-element.42) | copy-start | bytes 2359300
  261.5 3.5 %copy-start.2 = (f32[2,48,2048]{2,1,0:T(8,128)S(1)}, f32[2,48,2048]{2,1,0:T(8,128)}, u32[]{:S(2)}) copy-start(f32[2,48,2048]{2,1,0:T(8,128)} %get-tuple-element.43) | copy-start | bytes 2359300
  261.5 4.4 %copy-start.1 = (f32[2,128,768]{2,1,0:T(8,128)S(1)}, f32[2,128,768]{2,1,0:T(8,128)}, u32[]{:S(2)}) copy-start(f32[2,128,768]{2,1,0:T(8,128)} %get-tuple-element.44) | copy-start | bytes 2359300
